TPU v7x, 16 devices: a 4x2x1 block of a 4x4x8 slice. The times are simulated.
16 devices in a mesh: dp: 2 (over y, z), row: 8 (over x, core).
Axes of the slice: x: 4, y: 2, z: 1, core: 2. Of those that a mesh axis runs over, the one named last changes fastest.
The devices are a block of a 4x4x8 slice.
Arguments:
- adjacency: bfloat16 [32768, 16384], P(('dp', 'row')), parts along dimension 0
- features: bfloat16 [32768, 602], P(('dp', 'row')), parts along dimension 0
- w_first: bfloat16 [602, 256], replicated
- w_second: bfloat16 [256, 41], replicated
Outputs:
- output: float32 [32768, 41], P(('dp', 'row')), parts along dimension 0
There are 2 independent parts. A program takes and returns all parts, laid end to end along the dimension named above; an argument that names none is the same for every part.
All inputs are finite; a program needn't handle non-finite values.
Results may differ from a plain program's by a relative error of at most 0.00189754.
Values are sent between devices in bfloat16 or wider.
A program may use at most 768 MiB of HBM per device.

v0:
```python
import jax
import jax.numpy as jnp
from jax import lax
from jax.sharding import PartitionSpec as P, NamedSharding


def solution(mesh):
    row_spec = P(('dp', 'row'), None)
    full_spec = P(None, None)

    def per_device(adj_rows, feat_rows, w_first, w_second):
        z_first = jnp.dot(feat_rows, w_first, preferred_element_type=jnp.float32).astype(jnp.bfloat16)
        z_gathered = lax.all_gather(z_first, 'row', axis=0, tiled=True)
        hidden = jnp.maximum(jnp.dot(adj_rows, z_gathered, preferred_element_type=jnp.float32), 0.0).astype(jnp.bfloat16)
        z_second = jnp.dot(hidden, w_second, preferred_element_type=jnp.float32).astype(jnp.bfloat16)
        z_all = lax.all_gather(z_second, 'row', axis=0, tiled=True)
        return jnp.maximum(jnp.dot(adj_rows, z_all, preferred_element_type=jnp.float32), 0.0)

    return jax.shard_map(per_device, mesh=mesh, in_specs=(row_spec, row_spec, full_spec, full_spec), out_specs=row_spec, check_vma=False)
```

profile of v0, /device:TPU:112, one launch (start us, length us, event | category | flops | bytes accessed | tf_op | source)
XLA Modules:
  0.0 144.3 jit_solution(7986216847187137786)
XLA Ops:
  6.5 0.0 copy-start
  6.6 0.0 all-gather.3.cloned.1.call-start
  6.6 1.7 %copy-done = bf16[2048,602]{0,1:T(8,128)(2,1)S(1)} copy-done((bf16[2048,602]{0,1:T(8,128)(2,1)S(1)}, bf16[2048,602]{0,1:T(8,128)(2,1)}, u32[]{:S(2)}) %copy-start) | copy-done | bytes 2465816
  8.3 3.1 %convolution_convert_fusion = bf16[2048,256]{1,0:T(8,128)(2,1)} fusion(bf16[2048,602]{0,1:T(8,128)(2,1)S(1)} %copy-done, bf16[602,256]{1,0:T(8,128)(2,1)} %param.6), kind=kOutput, calls=%fused_computation.1 | convolution fusion | flops 631767040 | bytes 3822592 | tf_op jit(solution)/shard_map/dot_general | solution.py:12
  11.3 0.1 all-gather.3.cloned.1.call-update
  11.4 0.1 all-gather.5.cloned.1.call-start
  11.5 48.4 %all-gather.3.cloned.1.call-done = bf16[16384,256]{1,0:T(8,128)(2,1)} async-done(((bf16[2048,256]{1,0:T(8,128)(2,1)}), bf16[16384,256]{1,0:T(8,128)(2,1)}) %all-gather.3.cloned.1.call-update) | async-done | bytes 8388624 | tf_op jit(solution)/shard_map/all_gather | solution.py:13
  59.8 27.5 %fusion = bf16[256,2048]{1,0:T(8,128)(2,1)S(1)} fusion(bf16[16384,256]{1,0:T(8,128)(2,1)} %all-gather.3.cloned.1.call-done, bf16[2048,16384]{1,0:T(8,128)(2,1)} %param.4), kind=kOutput, calls=%fused_computation.2 | convolution fusion | flops 17180917760 | bytes 76546048 | tf_op jit(solution)/shard_map/dot_general | solution.py:14
  87.4 1.7 %convolution_convert_fusion.1 = bf16[2048,41]{0,1:T(8,128)(2,1)} fusion(bf16[256,2048]{1,0:T(8,128)(2,1)S(1)} %fusion, bf16[256,41]{0,1:T(8,128)(2,1)} %param.7), kind=kOutput, calls=%fused_computation.5 | convolution fusion | flops 43075584 | bytes 1237504 | tf_op jit(solution)/shard_map/dot_general | solution.py:15
  89.1 0.1 all-gather.5.cloned.1.call-update
  89.2 20.6 %all-gather.5.cloned.1.call-done = bf16[16384,41]{0,1:T(8,128)(2,1)} async-done(((bf16[2048,41]{0,1:T(8,128)(2,1)}), bf16[16384,41]{0,1:T(8,128)(2,1)}) %all-gather.5.cloned.1.call-update) | async-done | bytes 1343504 | tf_op jit(solution)/shard_map/all_gather | solution.py:16
  109.8 27.7 %fusion.1 = f32[2048,41]{0,1:T(8,128)} fusion(bf16[16384,41]{0,1:T(8,128)(2,1)} %all-gather.5.cloned.1.call-done, bf16[2048,16384]{1,0:T(8,128)(2,1)} %param.4), kind=kOutput, calls=%fused_computation.4 | convolution fusion | flops 2751547392 | bytes 68788224 | tf_op jit(solution)/shard_map/dot_general | solution.py:17
Async XLA Ops:
  6.5 1.7 %copy-start = (bf16[2048,602]{0,1:T(8,128)(2,1)S(1)}, bf16[2048,602]{0,1:T(8,128)(2,1)}, u32[]{:S(2)}) copy-start(bf16[2048,602]{0,1:T(8,128)(2,1)} %param.5) | copy-start | bytes 7397380
  6.6 53.3 %all-gather.3.cloned.1.call-start = ((), (), s32[]{:S(2)}) async-start(), calls=%async_computation | async-start | bytes 9437184 | tf_op jit(solution)/shard_map/all_gather | solution.py:13
  11.4 98.4 %all-gather.5.cloned.1.call-start = ((), (), s32[]{:S(2)}) async-start(), calls=%async_computation.1 | async-start | bytes 1769472 | tf_op jit(solution)/shard_map/all_gather | solution.py:16
Sparse Core Ops, SparseCore 0:
  11.5 48.2 all-gather.2
  89.3 20.4 all-gather.4
where the time goes:
time: 145 us; the launch traced here: 144 us
  waiting for transfers between devices  69.1 us (48%)
  matrix products  60 us (41%)
  between operations  13.4 us (9%)
  local copies, waits for them, and re-layouts  1.7 us (1%)
    all_gather x1, waiting for transfers between devices, per_device(): z_gathered = lax.all_gather(z_first, 'row', axis=0, tiled=True)  48.4 us
    dot_general x1, matrix products, per_device(): jnp.dot(adj_rows, z_all, preferred_element_type=jnp.float32)  27.7 us
    dot_general x1, matrix products, per_device(): jnp.dot(adj_rows, z_gathered, preferred_element_type=jnp.float32)  27.5 us
    all_gather x1, waiting for transfers between devices, per_device(): z_all = lax.all_gather(z_second, 'row', axis=0, tiled=True)  20.6 us
    dot_general x1, matrix products, per_device(): jnp.dot(feat_rows, w_first, preferred_element_type=jnp.float32)  3.07 us
  transfers between devices with their start and end apart: 2, of which 2 were waited for; matrix products, arithmetic and copies ran while one was open for 0% of the time, Pallas kernels for 0%

commit v1 on v0

v1 whole, which is shorter than its diff:
```python
import functools

import jax
import jax.numpy as jnp
from jax import lax
from jax.experimental import pallas as pl
from jax.experimental.pallas import tpu as pltpu
from jax.sharding import PartitionSpec as P

MESH = pl.DeviceIdType.MESH
CORES = 2
TILE = 256
F32, BF16 = jnp.float32, jnp.bfloat16

OWN, SIB, LEFT, RIGHT, SLEFT, SRIGHT, FAR, SFAR = range(8)
BLOCKS = 8
H0_RING = 4


def kernel(n, a_hbm, h0_hbm, w0_hbm, w1_hbm, out_hbm, slab, acc, h0_buf, w0_buf, w1_buf, z1t, h2t,
           a_sem, h0_sem, w_sem, z_recv, z_send, y_recv, y_send, out_sem):
    chips = n // CORES
    me = lax.axis_index("row")
    chip, core = me // CORES, me % CORES
    rows = acc.shape[0]
    pieces = rows // TILE
    half = pieces // 2
    zbase = slab.shape[0] - BLOCKS

    def device(step, flip):
        return (chip + step + chips) % chips * CORES + (core + flip) % CORES

    sib, left, right = device(0, 1), device(-1, 0), device(1, 0)

    def part(i):
        if isinstance(i, int):
            return pl.ds(i * TILE, TILE)
        return pl.ds(pl.multiple_of(i * TILE, TILE), TILE)

    def a_copy(owner, i, slot, sem):
        start = pl.multiple_of(owner * rows + i * TILE, TILE)
        return pltpu.make_async_copy(a_hbm.at[:, pl.ds(start, TILE)], slab.at[slot], a_sem.at[sem])

    def own_slab(i):
        return a_copy(me, i, i, i)

    def sib_slab(i):
        return a_copy(sib, i, pieces + i, pieces + i)

    def mid_slab(i, c):
        slot = 2 * pieces + 4 * i + c
        return a_copy(device(2 * (c % 2) - 1, c // 2), i, slot, slot)

    def far_slab(k, c):
        slot = 4 * k + c
        return a_copy(device(2, c // 2), 2 * k + c % 2, slot, slot)

    def z_ref(q, i):
        return slab.at[zbase + q, part(i)]

    def z_copy(src, dst, i, to, group):
        return pltpu.make_async_remote_copy(
            src_ref=z_ref(src, i), dst_ref=z_ref(dst, i), send_sem=z_send.at[group], recv_sem=z_recv.at[dst, i],
            device_id={"row": to}, device_id_type=MESH)

    def z_wait(q, i):
        z_copy(q, q, i, sib, 0).wait_recv()

    def z_sent(group, share):
        ref = slab.at[zbase, pl.ds(0, share * TILE)]
        pltpu.make_async_remote_copy(
            src_ref=ref, dst_ref=ref, send_sem=z_send.at[group], recv_sem=z_recv.at[0, 0],
            device_id={"row": sib}, device_id_type=MESH).wait_send()

    def y_copy(src, dst, h, to, group):
        return pltpu.make_async_remote_copy(
            src_ref=z1t.at[src, h], dst_ref=z1t.at[dst, h], send_sem=y_send.at[group, h], recv_sem=y_recv.at[dst, h],
            device_id={"row": to}, device_id_type=MESH)

    def y_wait(q, h):
        y_copy(q, q, h, sib, 0).wait_recv()

    def h0_copy(i):
        return pltpu.make_async_copy(h0_hbm.at[:, part(i)], h0_buf.at[i % H0_RING], h0_sem.at[i % H0_RING])

    w0_copy = pltpu.make_async_copy(w0_hbm, w0_buf, w_sem.at[0])
    w1_copy = pltpu.make_async_copy(w1_hbm, w1_buf, w_sem.at[1])
    w0_copy.start()
    for i in range(H0_RING):
        h0_copy(i).start()
    w1_copy.start()

    barrier = pltpu.get_barrier_semaphore()
    for peer in (sib, left, right):
        pl.semaphore_signal(barrier, inc=1, device_id={"row": peer}, device_id_type=MESH)

    @pl.loop(0, pieces)
    def _(i):
        own_slab(i).start()

    acc[...] = jnp.zeros_like(acc)
    w0_copy.wait()
    pl.semaphore_wait(barrier, 3)

    def send_own(i):
        z_copy(OWN, SIB, i, sib, 0).start()
        z_copy(OWN, LEFT, i, right, 1).start()
        z_copy(OWN, RIGHT, i, left, 2).start()

    @pl.loop(0, pieces)
    def _(i):
        h0_copy(i).wait()
        z = lax.dot_general(h0_buf[i % H0_RING], w0_buf[...], (((0,), (0,)), ((), ())), preferred_element_type=F32)
        slab[zbase + OWN, part(i)] = z.astype(BF16)

        @pl.when(i + H0_RING < pieces)
        def _():
            h0_copy(i + H0_RING).start()

        @pl.when(i > 0)
        def _():
            send_own(i - 1)

    @pl.loop(0, pieces)
    def _(i):
        sib_slab(i).start()

    w1_copy.wait()
    send_own(pieces - 1)

    def multiply(slot0, q0, i0, slot1, q1, i1):
        @pl.loop(0, pieces // 4)
        def _(jj):
            for u in range(4):
                r = part(4 * jj + u)
                acc[r, :] += (
                    jnp.dot(slab[slot0, r, :], slab[zbase + q0, part(i0)], preferred_element_type=F32)
                    + jnp.dot(slab[slot1, r, :], slab[zbase + q1, part(i1)], preferred_element_type=F32))

    @pl.loop(0, pieces // 2)
    def _(k):
        for u in range(2):
            own_slab(2 * k + u).wait()
            mid_slab((2 * k + u) // 4, (2 * k + u) % 4).start()
        multiply(2 * k, OWN, 2 * k, 2 * k + 1, OWN, 2 * k + 1)

    @pl.loop(0, pieces // 2)
    def _(k):
        for u in range(2):
            sib_slab(2 * k + u).wait()
            z_wait(SIB, 2 * k + u)
            mid_slab((pieces + 2 * k + u) // 4, (2 * k + u) % 4).start()
        multiply(pieces + 2 * k, SIB, 2 * k, pieces + 2 * k + 1, SIB, 2 * k + 1)

    def mid(i, even, ahead):
        base = 2 * pieces + 4 * i
        z_wait(LEFT, i)
        z_copy(LEFT, SLEFT, i, sib, 3).start()
        if even:
            z_copy(LEFT, FAR, i, right, 5).start()
        z_wait(RIGHT, i)
        z_copy(RIGHT, SRIGHT, i, sib, 4).start()
        if not even:
            z_copy(RIGHT, FAR, i, left, 6).start()
        for c in range(4):
            mid_slab(i, c).wait()
            ahead(c)
        multiply(base, LEFT, i, base + 1, RIGHT, i)
        z_wait(SLEFT, i)
        z_wait(SRIGHT, i)
        multiply(base + 2, SLEFT, i, base + 3, SRIGHT, i)

    @pl.loop(0, pieces // 4)
    def _(k):
        for u in range(2):
            i = 2 * k + u
            mid(i, u == 0, lambda c: mid_slab(i + half, c).start())

    @pl.loop(pieces // 4, pieces // 2)
    def _(k):
        for u in range(2):
            i = 2 * k + u
            mid(i, u == 0, lambda c: far_slab(i - half, c).start())

    z_sent(0, pieces)
    z_sent(1, pieces)
    z_sent(2, pieces)
    home = [zbase + q for q in (OWN, SIB, SLEFT, SRIGHT, LEFT, RIGHT, FAR, SFAR)]

    def again(owner, i):
        return a_copy(owner, i, home[i], 2 * pieces + i)

    for i in range(4):
        again(me, i).start()

    @pl.loop(0, pieces // 2)
    def _(k):
        for u in range(2):
            z_wait(FAR, 2 * k + u)
            z_copy(FAR, SFAR, 2 * k + u, sib, 7).start()
        for c in range(4):
            far_slab(k, c).wait()
        multiply(4 * k, FAR, 2 * k, 4 * k + 1, FAR, 2 * k + 1)
        for u in range(2):
            z_wait(SFAR, 2 * k + u)
        multiply(4 * k + 2, SFAR, 2 * k, 4 * k + 3, SFAR, 2 * k + 1)

    z_sent(3, pieces)
    z_sent(4, pieces)
    z_sent(5, pieces // 2)
    z_sent(6, pieces // 2)
    z_sent(7, pieces)
    for i in range(4, pieces):
        again(me, i).start()

    @pl.loop(0, pieces // 2)
    def _(jj):
        for u in range(2):
            j = 2 * jj + u
            hidden = jnp.maximum(acc[part(j), :], 0.0).astype(BF16)
            y = lax.dot_general(w1_buf[...], hidden, (((1,), (1,)), ((), ())), preferred_element_type=F32)
            z1t[OWN, j // half, j % half] = y.astype(BF16)

    y_copy(OWN, LEFT, 0, right, 1).start()
    y_copy(OWN, RIGHT, 1, left, 2).start()
    y_copy(OWN, SIB, 0, sib, 0).start()
    y_copy(OWN, SIB, 1, sib, 0).start()
    y_copy(OWN, LEFT, 1, right, 1).start()
    y_copy(OWN, RIGHT, 0, left, 2).start()

    h2t[...] = jnp.zeros_like(h2t)

    def second(q, h, slots):
        @pl.loop(0, pieces // 2)
        def _(jj):
            for u in range(2):
                j = 2 * jj + u
                total = h2t[j]
                for i in range(half):
                    total += lax.dot_general(
                        z1t[q, h, i], slab[slots[i], part(j), :], (((1,), (1,)), ((), ())),
                        preferred_element_type=F32)
                h2t[j] = total

    def mid_slots(c, h):
        return [2 * pieces + 4 * (h * half + i) + c for i in range(half)]

    def far_slots(c, h):
        return [4 * ((h * half + i) // 2) + 2 * c + (h * half + i) % 2 for i in range(half)]

    for h in range(2):
        for i in range(half):
            again(me, h * half + i).wait()
        second(OWN, h, home[h * half:(h + 1) * half])
        for i in range(half):
            again(sib, h * half + i).start()

    y_wait(LEFT, 0)
    y_copy(LEFT, FAR, 0, right, 5).start()
    y_copy(LEFT, SLEFT, 0, sib, 3).start()
    y_wait(RIGHT, 1)
    y_copy(RIGHT, FAR, 1, left, 6).start()
    y_copy(RIGHT, SRIGHT, 1, sib, 4).start()
    for h in range(2):
        y_wait(SIB, h)
        for i in range(half):
            again(sib, h * half + i).wait()
        second(SIB, h, home[h * half:(h + 1) * half])
    y_wait(LEFT, 1)
    y_copy(LEFT, SLEFT, 1, sib, 3).start()
    y_wait(RIGHT, 0)
    y_copy(RIGHT, SRIGHT, 0, sib, 4).start()
    second(LEFT, 0, mid_slots(0, 0))
    second(RIGHT, 1, mid_slots(1, 1))
    second(LEFT, 1, mid_slots(0, 1))
    y_wait(FAR, 0)
    y_copy(FAR, SFAR, 0, sib, 7).start()
    y_wait(FAR, 1)
    y_copy(FAR, SFAR, 1, sib, 7).start()
    second(RIGHT, 0, mid_slots(1, 0))
    for h in (0, 1):
        y_wait(SLEFT, h)
        second(SLEFT, h, mid_slots(2, h))
    for h in (1, 0):
        y_wait(SRIGHT, h)
        second(SRIGHT, h, mid_slots(3, h))
    second(FAR, 0, far_slots(0, 0))
    second(FAR, 1, far_slots(0, 1))
    for h in range(2):
        y_wait(SFAR, h)
        second(SFAR, h, far_slots(1, h))

    h2t[...] = jnp.maximum(h2t[...], 0.0)
    out_copies = [pltpu.make_async_copy(h2t.at[j], out_hbm.at[:, part(j)], out_sem.at[j]) for j in range(pieces)]
    for copy in out_copies:
        copy.start()
    for group in (0, 1, 2, 3, 4, 7):
        for h in range(2):
            y_copy(OWN, OWN, h, sib, group).wait_send()
    y_copy(OWN, OWN, 0, sib, 5).wait_send()
    y_copy(OWN, OWN, 1, sib, 6).wait_send()
    for copy in out_copies:
        copy.wait()


def solution(mesh):
    n = mesh.shape["row"]
    row_spec = P(("dp", "row"), None)
    full_spec = P(None, None)

    def per_device(adjacency, features, w_first, w_second):
        rows, feat, hidden, classes = features.shape[0], features.shape[1], w_first.shape[1], w_second.shape[1]
        pieces = rows // TILE
        resident = adjacency.shape[1] // TILE - 2 * pieces
        flops = 2 * rows * adjacency.shape[1] * (hidden + classes)
        out = pl.pallas_call(
            functools.partial(kernel, n),
            name="gcn",
            out_shape=jax.ShapeDtypeStruct((classes, rows), F32),
            in_specs=[pl.BlockSpec(memory_space=pl.ANY)] * 4,
            out_specs=pl.BlockSpec(memory_space=pl.ANY),
            scratch_shapes=[
                pltpu.VMEM((resident + BLOCKS, rows, TILE), BF16),
                pltpu.VMEM((rows, hidden), F32),
                pltpu.VMEM((H0_RING, feat, TILE), BF16),
                pltpu.VMEM((feat, hidden), BF16),
                pltpu.VMEM((classes, hidden), BF16),
                pltpu.VMEM((BLOCKS, 2, pieces // 2, classes, TILE), BF16),
                pltpu.VMEM((pieces, classes, TILE), F32),
                pltpu.SemaphoreType.DMA((resident,)),
                pltpu.SemaphoreType.DMA((H0_RING,)),
                pltpu.SemaphoreType.DMA((2,)),
                pltpu.SemaphoreType.DMA((BLOCKS, pieces)),
                pltpu.SemaphoreType.DMA((BLOCKS,)),
                pltpu.SemaphoreType.DMA((BLOCKS, 2)),
                pltpu.SemaphoreType.DMA((BLOCKS, 2)),
                pltpu.SemaphoreType.DMA((pieces,)),
            ],
            compiler_params=pltpu.CompilerParams(
                collective_id=0, has_side_effects=True, vmem_limit_bytes=67_043_328),
            cost_estimate=pl.CostEstimate(
                flops=flops, bytes_accessed=2 * adjacency.size, transcendentals=0),
        )(adjacency, features.T, w_first, w_second.T)
        return out.T

    return jax.shard_map(
        per_device, mesh=mesh, in_specs=(row_spec, row_spec, full_spec, full_spec), out_specs=row_spec,
        check_vma=False)
```

time: 145 us -> 77.2 us (0.53)
  Pallas kernels: 0 us -> 75.3 us
  waiting for transfers between devices: 69.1 us -> 0 us
  matrix products: 60 us -> 0 us
  between operations: 13.4 us -> 0.01 us
    pallas_call x0 -> x1, Pallas kernels: none -> 75.3 us  [per_device(): pl.pallas_call(functools.partial(kernel, n), name='gcn', out_shape=jax.Sh...]
    all_gather x2 -> x0, waiting for transfers between devices: 69 us -> none  [the longest x1 48.4 us: per_device(): z_gathered = lax.all_gather(z_first, 'row', axis=0, tiled=True)]
    dot_general x4 -> x0, matrix products: 60 us -> none  [the longest x1 27.7 us: per_device(): jnp.dot(adj_rows, z_all, preferred_element_type=jnp.float32)]
  transfers between devices with their start and end apart: 2 -> 0, of which waited for: 2 -> 0; matrix products, arithmetic and copies ran while one was open for 0% -> 0% of each run, Pallas kernels for 0% -> 0%
where the time goes in v1:
time: 77.2 us; the launch traced here: 77.1 us
  Pallas kernels  75.3 us (98%)
  local copies, waits for them, and re-layouts  1.77 us (2%)
    pallas_call x1, Pallas kernels, per_device(): pl.pallas_call(functools.partial(kernel, n), name='gcn', out_shape=jax.Sh...  75.3 us
    unnamed x1, local copies, waits for them, and re-layouts  1.77 us

profile of v1, /device:TPU:112, one launch (start us, length us, event | category | flops | bytes accessed | tf_op | source)
XLA Modules:
  0.0 77.1 jit_solution(3479612146097351549)
XLA Ops:
  0.0 75.3 %gcn.1 = f32[41,2048]{1,0:T(8,128)} custom-call(bf16[2048,16384]{1,0:T(8,128)(2,1)} %a_hbm.1, bf16[602,2048]{1,0:T(8,128)(2,1)} %bitcast.4, bf16[602,256]{1,0:T(8,128)(2,1)} %w0_hbm.1, bf16[41,256]{1,0:T(8,128)(2,1)} %bitcast.5), custom_call_target="tpu_custom_call" | custom-call | flops 19931332608 | bytes 67108864 | tf_op jit(solution)/shard_map/gcn/pallas_call | solution.py:316
  75.3 1.8 %copy.6 = f32[2048,41]{0,1:T(8,128)} copy(f32[2048,41]{0,1:T(8,128)} %bitcast.3) | data formatting | bytes 671744

commit v2 on v1

--- a/solution.py
+++ b/solution.py
@@ -12,7 +12,7 @@
 TILE = 256
 F32, BF16 = jnp.float32, jnp.bfloat16
 
-OWN, SIB, LEFT, RIGHT, SLEFT, SRIGHT, FAR, SFAR = range(8)
+OWN, SIB, SLEFT, SRIGHT, LEFT, RIGHT, FAR, SFAR = range(8)
 BLOCKS = 8
 H0_RING = 4
 
@@ -26,6 +26,7 @@
     pieces = rows // TILE
     half = pieces // 2
     zbase = slab.shape[0] - BLOCKS
+    classes = w1_buf.shape[0]
 
     def device(step, flip):
         return (chip + step + chips) % chips * CORES + (core + flip) % CORES
@@ -129,13 +130,11 @@
     send_own(pieces - 1)
 
     def multiply(slot0, q0, i0, slot1, q1, i1):
-        @pl.loop(0, pieces // 4)
-        def _(jj):
-            for u in range(4):
-                r = part(4 * jj + u)
-                acc[r, :] += (
-                    jnp.dot(slab[slot0, r, :], slab[zbase + q0, part(i0)], preferred_element_type=F32)
-                    + jnp.dot(slab[slot1, r, :], slab[zbase + q1, part(i1)], preferred_element_type=F32))
+        for j in range(pieces):
+            r = part(j)
+            acc[r, :] += (
+                jnp.dot(slab[slot0, r, :], slab[zbase + q0, part(i0)], preferred_element_type=F32)
+                + jnp.dot(slab[slot1, r, :], slab[zbase + q1, part(i1)], preferred_element_type=F32))
 
     @pl.loop(0, pieces // 2)
     def _(k):
@@ -185,10 +184,8 @@
     z_sent(0, pieces)
     z_sent(1, pieces)
     z_sent(2, pieces)
-    home = [zbase + q for q in (OWN, SIB, SLEFT, SRIGHT, LEFT, RIGHT, FAR, SFAR)]
-
     def again(owner, i):
-        return a_copy(owner, i, home[i], 2 * pieces + i)
+        return a_copy(owner, i, zbase + i, 2 * pieces + i)
 
     for i in range(4):
         again(me, i).start()
@@ -228,69 +225,67 @@
     y_copy(OWN, LEFT, 1, right, 1).start()
     y_copy(OWN, RIGHT, 0, left, 2).start()
 
-    h2t[...] = jnp.zeros_like(h2t)
-
-    def second(q, h, slots):
-        @pl.loop(0, pieces // 2)
-        def _(jj):
-            for u in range(2):
-                j = 2 * jj + u
-                total = h2t[j]
-                for i in range(half):
-                    total += lax.dot_general(
-                        z1t[q, h, i], slab[slots[i], part(j), :], (((1,), (1,)), ((), ())),
-                        preferred_element_type=F32)
-                h2t[j] = total
-
-    def mid_slots(c, h):
-        return [2 * pieces + 4 * (h * half + i) + c for i in range(half)]
-
-    def far_slots(c, h):
-        return [4 * ((h * half + i) // 2) + 2 * c + (h * half + i) % 2 for i in range(half)]
+    def second(work, first=False):
+        for j in range(pieces):
+            total = None
+            for q, h, i, slot in work:
+                term = lax.dot_general(
+                    slab[slot, part(j), :], z1t[q, h, i], (((1,), (1,)), ((), ())), preferred_element_type=F32)
+                total = term if total is None else total + term
+            if first:
+                acc[part(j), 0:classes] = total
+            else:
+                acc[part(j), 0:classes] += total
+
+    def pieces_of(q, h, slot_of):
+        return [(q, h, i, slot_of(h * half + i)) for i in range(half)]
+
+    def home(i):
+        return zbase + i
+
+    def mid_slot(c):
+        return lambda i: 2 * pieces + 4 * i + c
+
+    def far_slot(c):
+        return lambda i: 4 * (i // 2) + 2 * c + i % 2
 
     for h in range(2):
         for i in range(half):
             again(me, h * half + i).wait()
-        second(OWN, h, home[h * half:(h + 1) * half])
+        second(pieces_of(OWN, h, home), first=h == 0)
         for i in range(half):
             again(sib, h * half + i).start()
-
     y_wait(LEFT, 0)
     y_copy(LEFT, FAR, 0, right, 5).start()
     y_copy(LEFT, SLEFT, 0, sib, 3).start()
     y_wait(RIGHT, 1)
     y_copy(RIGHT, FAR, 1, left, 6).start()
     y_copy(RIGHT, SRIGHT, 1, sib, 4).start()
-    for h in range(2):
-        y_wait(SIB, h)
-        for i in range(half):
-            again(sib, h * half + i).wait()
-        second(SIB, h, home[h * half:(h + 1) * half])
+    second(pieces_of(LEFT, 0, mid_slot(0)) + pieces_of(RIGHT, 1, mid_slot(1)))
     y_wait(LEFT, 1)
     y_copy(LEFT, SLEFT, 1, sib, 3).start()
     y_wait(RIGHT, 0)
     y_copy(RIGHT, SRIGHT, 0, sib, 4).start()
-    second(LEFT, 0, mid_slots(0, 0))
-    second(RIGHT, 1, mid_slots(1, 1))
-    second(LEFT, 1, mid_slots(0, 1))
-    y_wait(FAR, 0)
-    y_copy(FAR, SFAR, 0, sib, 7).start()
-    y_wait(FAR, 1)
-    y_copy(FAR, SFAR, 1, sib, 7).start()
-    second(RIGHT, 0, mid_slots(1, 0))
-    for h in (0, 1):
+    for h in range(2):
+        y_wait(SIB, h)
+    for i in range(pieces):
+        again(sib, i).wait()
+    second(pieces_of(SIB, 0, home) + pieces_of(SIB, 1, home))
+    second(pieces_of(LEFT, 1, mid_slot(0)) + pieces_of(RIGHT, 0, mid_slot(1)))
+    for h in range(2):
+        y_wait(FAR, h)
+        y_copy(FAR, SFAR, h, sib, 7).start()
+    for h in range(2):
         y_wait(SLEFT, h)
-        second(SLEFT, h, mid_slots(2, h))
-    for h in (1, 0):
-        y_wait(SRIGHT, h)
-        second(SRIGHT, h, mid_slots(3, h))
-    second(FAR, 0, far_slots(0, 0))
-    second(FAR, 1, far_slots(0, 1))
+        y_wait(SRIGHT, 1 - h)
+        second(pieces_of(SLEFT, h, mid_slot(2)) + pieces_of(SRIGHT, 1 - h, mid_slot(3)))
+    second(pieces_of(FAR, 0, far_slot(0)) + pieces_of(FAR, 1, far_slot(0)))
     for h in range(2):
         y_wait(SFAR, h)
-        second(SFAR, h, far_slots(1, h))
-
-    h2t[...] = jnp.maximum(h2t[...], 0.0)
+    second(pieces_of(SFAR, 0, far_slot(1)) + pieces_of(SFAR, 1, far_slot(1)))
+    for j in range(pieces):
+        h2t[j] = jnp.maximum(acc[part(j), 0:128].T[0:classes], 0.0)
+
     out_copies = [pltpu.make_async_copy(h2t.at[j], out_hbm.at[:, part(j)], out_sem.at[j]) for j in range(pieces)]
     for copy in out_copies:
         copy.start()

time: 77.2 us -> 69.4 us (0.90)
  Pallas kernels: 75.3 us -> 67.5 us
    pallas_call x1, Pallas kernels: 75.3 us -> 67.5 us  [per_device(): pl.pallas_call(functools.partial(kernel, n), name='gcn', out_shape=jax.Sh...]
where the time goes in v2:
time: 69.4 us; the launch traced here: 69.3 us
  Pallas kernels  67.5 us (97%)
  local copies, waits for them, and re-layouts  1.77 us (3%)
    pallas_call x1, Pallas kernels, per_device(): pl.pallas_call(functools.partial(kernel, n), name='gcn', out_shape=jax.Sh...  67.5 us
    unnamed x1, local copies, waits for them, and re-layouts  1.77 us

profile of v2, /device:TPU:112, one launch (start us, length us, event | category | flops | bytes accessed | tf_op | source)
XLA Modules:
  0.0 69.3 jit_solution(3517884181738650933)
XLA Ops:
  0.0 67.5 %gcn.1 = f32[41,2048]{1,0:T(8,128)} custom-call(bf16[2048,16384]{1,0:T(8,128)(2,1)} %a_hbm.1, bf16[602,2048]{1,0:T(8,128)(2,1)} %bitcast.4, bf16[602,256]{1,0:T(8,128)(2,1)} %w0_hbm.1, bf16[41,256]{1,0:T(8,128)(2,1)} %bitcast.5), custom_call_target="tpu_custom_call" | custom-call | flops 19931332608 | bytes 67108864 | tf_op jit(solution)/shard_map/gcn/pallas_call | solution.py:311
  67.5 1.8 %copy.6 = f32[2048,41]{0,1:T(8,128)} copy(f32[2048,41]{0,1:T(8,128)} %bitcast.3) | data formatting | bytes 671744

commit v3 on v2

--- a/solution.py
+++ b/solution.py
@@ -15,9 +15,10 @@
 OWN, SIB, SLEFT, SRIGHT, LEFT, RIGHT, FAR, SFAR = range(8)
 BLOCKS = 8
 H0_RING = 4
-
-
-def kernel(n, a_hbm, h0_hbm, w0_hbm, w1_hbm, out_hbm, slab, acc, h0_buf, w0_buf, w1_buf, z1t, h2t,
+LANES = 128
+
+
+def kernel(n, a_hbm, h0_hbm, w0_hbm, w1_hbm, out_hbm, slab, acc, h0_buf, w0_buf, w1_buf, w1_pad, z1t, h2t, out_buf,
            a_sem, h0_sem, w_sem, z_recv, z_send, y_recv, y_send, out_sem):
     chips = n // CORES
     me = lax.axis_index("row")
@@ -100,6 +101,7 @@
         own_slab(i).start()
 
     acc[...] = jnp.zeros_like(acc)
+    w1_pad[...] = jnp.zeros_like(w1_pad)
     w0_copy.wait()
     pl.semaphore_wait(barrier, 3)
 
@@ -127,21 +129,24 @@
         sib_slab(i).start()
 
     w1_copy.wait()
+    w1_pad[0:classes] = w1_buf[...]
     send_own(pieces - 1)
 
-    def multiply(slot0, q0, i0, slot1, q1, i1):
-        for j in range(pieces):
-            r = part(j)
-            acc[r, :] += (
-                jnp.dot(slab[slot0, r, :], slab[zbase + q0, part(i0)], preferred_element_type=F32)
-                + jnp.dot(slab[slot1, r, :], slab[zbase + q1, part(i1)], preferred_element_type=F32))
+    def multiply(slot0, q0, i0, slot1, q1, i1, keep=True):
+        slots, z = (slot0, slot1), (z_ref(q0, i0), z_ref(q1, i1))
+        for j in range(pieces + 1):
+            for u in range(2):
+                if j < pieces:
+                    acc[part(j), :] += jnp.dot(slab[slots[u], part(j), :], z[u][...], preferred_element_type=F32)
+                if j > 0 and keep:
+                    slab[slots[u], part(j - 1), :] = slab[slots[u], part(j - 1), :].T
 
     @pl.loop(0, pieces // 2)
     def _(k):
         for u in range(2):
             own_slab(2 * k + u).wait()
             mid_slab((2 * k + u) // 4, (2 * k + u) % 4).start()
-        multiply(2 * k, OWN, 2 * k, 2 * k + 1, OWN, 2 * k + 1)
+        multiply(2 * k, OWN, 2 * k, 2 * k + 1, OWN, 2 * k + 1, keep=False)
 
     @pl.loop(0, pieces // 2)
     def _(k):
@@ -149,7 +154,7 @@
             sib_slab(2 * k + u).wait()
             z_wait(SIB, 2 * k + u)
             mid_slab((pieces + 2 * k + u) // 4, (2 * k + u) % 4).start()
-        multiply(pieces + 2 * k, SIB, 2 * k, pieces + 2 * k + 1, SIB, 2 * k + 1)
+        multiply(pieces + 2 * k, SIB, 2 * k, pieces + 2 * k + 1, SIB, 2 * k + 1, keep=False)
 
     def mid(i, even, ahead):
         base = 2 * pieces + 4 * i
@@ -190,17 +195,22 @@
     for i in range(4):
         again(me, i).start()
 
-    @pl.loop(0, pieces // 2)
-    def _(k):
+    def far(k, keep):
         for u in range(2):
             z_wait(FAR, 2 * k + u)
             z_copy(FAR, SFAR, 2 * k + u, sib, 7).start()
         for c in range(4):
             far_slab(k, c).wait()
-        multiply(4 * k, FAR, 2 * k, 4 * k + 1, FAR, 2 * k + 1)
+        multiply(4 * k, FAR, 2 * k, 4 * k + 1, FAR, 2 * k + 1, keep)
         for u in range(2):
             z_wait(SFAR, 2 * k + u)
-        multiply(4 * k + 2, SFAR, 2 * k, 4 * k + 3, SFAR, 2 * k + 1)
+        multiply(4 * k + 2, SFAR, 2 * k, 4 * k + 3, SFAR, 2 * k + 1, keep)
+
+    @pl.loop(0, pieces // 2 - 1)
+    def _(k):
+        far(k, True)
+
+    far(pieces // 2 - 1, False)
 
     z_sent(3, pieces)
     z_sent(4, pieces)
@@ -210,13 +220,10 @@
     for i in range(4, pieces):
         again(me, i).start()
 
-    @pl.loop(0, pieces // 2)
-    def _(jj):
-        for u in range(2):
-            j = 2 * jj + u
-            hidden = jnp.maximum(acc[part(j), :], 0.0).astype(BF16)
-            y = lax.dot_general(w1_buf[...], hidden, (((1,), (1,)), ((), ())), preferred_element_type=F32)
-            z1t[OWN, j // half, j % half] = y.astype(BF16)
+    for j in range(pieces):
+        hidden = jnp.maximum(acc[part(j), :], 0.0).astype(BF16)
+        y = lax.dot_general(w1_pad[...], hidden, (((1,), (1,)), ((), ())), preferred_element_type=F32)
+        z1t[OWN, j // half, j % half] = y.astype(BF16)
 
     y_copy(OWN, LEFT, 0, right, 1).start()
     y_copy(OWN, RIGHT, 1, left, 2).start()
@@ -229,13 +236,25 @@
         for j in range(pieces):
             total = None
             for q, h, i, slot in work:
+                y = jnp.concatenate([z1t[q, h, i], jnp.zeros((LANES - z1t.shape[3], TILE), BF16)], axis=0)
                 term = lax.dot_general(
-                    slab[slot, part(j), :], z1t[q, h, i], (((1,), (1,)), ((), ())), preferred_element_type=F32)
+                    slab[slot, part(j), :], y, (((1,), (1,)), ((), ())), preferred_element_type=F32)
                 total = term if total is None else total + term
             if first:
-                acc[part(j), 0:classes] = total
+                acc[part(j), 0:LANES] = total
             else:
-                acc[part(j), 0:classes] += total
+                acc[part(j), 0:LANES] += total
+
+    def second_turned(work, first=False):
+        for j in range(pieces):
+            total = None
+            for q, h, i, slot in work:
+                term = jnp.dot(z1t[q, h, i], slab[slot, part(j), :], preferred_element_type=F32)
+                total = term if total is None else total + term
+            if first:
+                h2t[j] = total
+            else:
+                h2t[j] += total
 
     def pieces_of(q, h, slot_of):
         return [(q, h, i, slot_of(h * half + i)) for i in range(half)]
@@ -261,7 +280,7 @@
     y_wait(RIGHT, 1)
     y_copy(RIGHT, FAR, 1, left, 6).start()
     y_copy(RIGHT, SRIGHT, 1, sib, 4).start()
-    second(pieces_of(LEFT, 0, mid_slot(0)) + pieces_of(RIGHT, 1, mid_slot(1)))
+    second_turned(pieces_of(LEFT, 0, mid_slot(0)) + pieces_of(RIGHT, 1, mid_slot(1)), first=True)
     y_wait(LEFT, 1)
     y_copy(LEFT, SLEFT, 1, sib, 3).start()
     y_wait(RIGHT, 0)
@@ -271,22 +290,25 @@
     for i in range(pieces):
         again(sib, i).wait()
     second(pieces_of(SIB, 0, home) + pieces_of(SIB, 1, home))
-    second(pieces_of(LEFT, 1, mid_slot(0)) + pieces_of(RIGHT, 0, mid_slot(1)))
+    second_turned(pieces_of(LEFT, 1, mid_slot(0)) + pieces_of(RIGHT, 0, mid_slot(1)))
     for h in range(2):
         y_wait(FAR, h)
         y_copy(FAR, SFAR, h, sib, 7).start()
     for h in range(2):
         y_wait(SLEFT, h)
         y_wait(SRIGHT, 1 - h)
-        second(pieces_of(SLEFT, h, mid_slot(2)) + pieces_of(SRIGHT, 1 - h, mid_slot(3)))
-    second(pieces_of(FAR, 0, far_slot(0)) + pieces_of(FAR, 1, far_slot(0)))
+        second_turned(pieces_of(SLEFT, h, mid_slot(2)) + pieces_of(SRIGHT, 1 - h, mid_slot(3)))
+    far_work = pieces_of(FAR, 0, far_slot(0)) + pieces_of(FAR, 1, far_slot(0))
+    sfar_work = pieces_of(SFAR, 0, far_slot(1)) + pieces_of(SFAR, 1, far_slot(1))
+    second_turned(far_work[:-2])
     for h in range(2):
         y_wait(SFAR, h)
-    second(pieces_of(SFAR, 0, far_slot(1)) + pieces_of(SFAR, 1, far_slot(1)))
+    second_turned(sfar_work[:-2])
+    second(far_work[-2:] + sfar_work[-2:])
     for j in range(pieces):
-        h2t[j] = jnp.maximum(acc[part(j), 0:128].T[0:classes], 0.0)
-
-    out_copies = [pltpu.make_async_copy(h2t.at[j], out_hbm.at[:, part(j)], out_sem.at[j]) for j in range(pieces)]
+        out_buf[j] = jnp.maximum(h2t[j, 0:classes] + acc[part(j), 0:LANES].T[0:classes], 0.0)
+
+    out_copies = [pltpu.make_async_copy(out_buf.at[j], out_hbm.at[:, part(j)], out_sem.at[j]) for j in range(pieces)]
     for copy in out_copies:
         copy.start()
     for group in (0, 1, 2, 3, 4, 7):
@@ -306,6 +328,7 @@
     def per_device(adjacency, features, w_first, w_second):
         rows, feat, hidden, classes = features.shape[0], features.shape[1], w_first.shape[1], w_second.shape[1]
         pieces = rows // TILE
+        padded = -(-classes // 16) * 16
         resident = adjacency.shape[1] // TILE - 2 * pieces
         flops = 2 * rows * adjacency.shape[1] * (hidden + classes)
         out = pl.pallas_call(
@@ -320,7 +343,9 @@
                 pltpu.VMEM((H0_RING, feat, TILE), BF16),
                 pltpu.VMEM((feat, hidden), BF16),
                 pltpu.VMEM((classes, hidden), BF16),
-                pltpu.VMEM((BLOCKS, 2, pieces // 2, classes, TILE), BF16),
+                pltpu.VMEM((padded, hidden), BF16),
+                pltpu.VMEM((BLOCKS, 2, pieces // 2, padded, TILE), BF16),
+                pltpu.VMEM((pieces, padded, TILE), F32),
                 pltpu.VMEM((pieces, classes, TILE), F32),
                 pltpu.SemaphoreType.DMA((resident,)),
                 pltpu.SemaphoreType.DMA((H0_RING,)),

time: 69.4 us -> 64.7 us (0.932)
  Pallas kernels: 67.5 us -> 62.8 us
    pallas_call x1, Pallas kernels: 67.5 us -> 62.8 us  [per_device(): pl.pallas_call(functools.partial(kernel, n), name='gcn', out_shape=jax.Sh...]
where the time goes in v3:
time: 64.7 us; the launch traced here: 64.5 us
  Pallas kernels  62.8 us (97%)
  local copies, waits for them, and re-layouts  1.77 us (3%)
    pallas_call x1, Pallas kernels, per_device(): pl.pallas_call(functools.partial(kernel, n), name='gcn', out_shape=jax.Sh...  62.8 us
    unnamed x1, local copies, waits for them, and re-layouts  1.77 us

profile of v3, /device:TPU:112, one launch (start us, length us, event | category | flops | bytes accessed | tf_op | source)
XLA Modules:
  0.0 64.5 jit_solution(9147963841282650734)
XLA Ops:
  0.0 62.8 %gcn.1 = f32[41,2048]{1,0:T(8,128)} custom-call(bf16[2048,16384]{1,0:T(8,128)(2,1)} %a_hbm.1, bf16[602,2048]{1,0:T(8,128)(2,1)} %bitcast.4, bf16[602,256]{1,0:T(8,128)(2,1)} %w0_hbm.1, bf16[41,256]{1,0:T(8,128)(2,1)} %bitcast.5), custom_call_target="tpu_custom_call" | custom-call | flops 19931332608 | bytes 67108864 | tf_op jit(solution)/shard_map/gcn/pallas_call | solution.py:334
  62.8 1.8 %copy.6 = f32[2048,41]{0,1:T(8,128)} copy(f32[2048,41]{0,1:T(8,128)} %bitcast.3) | data formatting | bytes 671744

commit v4 on v3

--- a/solution.py
+++ b/solution.py
@@ -103,15 +103,13 @@
     acc[...] = jnp.zeros_like(acc)
     w1_pad[...] = jnp.zeros_like(w1_pad)
     w0_copy.wait()
-    pl.semaphore_wait(barrier, 3)
 
     def send_own(i):
         z_copy(OWN, SIB, i, sib, 0).start()
         z_copy(OWN, LEFT, i, right, 1).start()
         z_copy(OWN, RIGHT, i, left, 2).start()
 
-    @pl.loop(0, pieces)
-    def _(i):
+    def feature(i):
         h0_copy(i).wait()
         z = lax.dot_general(h0_buf[i % H0_RING], w0_buf[...], (((0,), (0,)), ((), ())), preferred_element_type=F32)
         slab[zbase + OWN, part(i)] = z.astype(BF16)
@@ -120,9 +118,13 @@
         def _():
             h0_copy(i + H0_RING).start()
 
-        @pl.when(i > 0)
-        def _():
-            send_own(i - 1)
+    feature(0)
+    pl.semaphore_wait(barrier, 3)
+
+    @pl.loop(1, pieces)
+    def _(i):
+        feature(i)
+        send_own(i - 1)
 
     @pl.loop(0, pieces)
     def _(i):
@@ -156,8 +158,7 @@
             mid_slab((pieces + 2 * k + u) // 4, (2 * k + u) % 4).start()
         multiply(pieces + 2 * k, SIB, 2 * k, pieces + 2 * k + 1, SIB, 2 * k + 1, keep=False)
 
-    def mid(i, even, ahead):
-        base = 2 * pieces + 4 * i
+    def front(i, even):
         z_wait(LEFT, i)
         z_copy(LEFT, SLEFT, i, sib, 3).start()
         if even:
@@ -166,51 +167,77 @@
         z_copy(RIGHT, SRIGHT, i, sib, 4).start()
         if not even:
             z_copy(RIGHT, FAR, i, left, 6).start()
-        for c in range(4):
+        for c in range(2):
             mid_slab(i, c).wait()
-            ahead(c)
+
+        @pl.when(i < half)
+        def _():
+            for c in range(4):
+                mid_slab(i + half, c).start()
+
+        @pl.when(i >= half)
+        def _():
+            for c in range(4):
+                far_slab(i - half, c).start()
+
+        base = 2 * pieces + 4 * i
         multiply(base, LEFT, i, base + 1, RIGHT, i)
+
+    def back(i):
+        for c in range(2, 4):
+            mid_slab(i, c).wait()
         z_wait(SLEFT, i)
         z_wait(SRIGHT, i)
+        base = 2 * pieces + 4 * i
         multiply(base + 2, SLEFT, i, base + 3, SRIGHT, i)
 
-    @pl.loop(0, pieces // 4)
+    @pl.loop(0, pieces // 2)
     def _(k):
+        front(2 * k, True)
+
+        @pl.when(k > 0)
+        def _():
+            back(2 * k - 1)
+
+        front(2 * k + 1, False)
+        back(2 * k)
+
+    def far_front(k, keep=True):
         for u in range(2):
-            i = 2 * k + u
-            mid(i, u == 0, lambda c: mid_slab(i + half, c).start())
-
-    @pl.loop(pieces // 4, pieces // 2)
-    def _(k):
+            z_wait(FAR, 2 * k + u)
+            z_copy(FAR, SFAR, 2 * k + u, sib, 7).start()
+        for c in range(2):
+            far_slab(k, c).wait()
+        multiply(4 * k, FAR, 2 * k, 4 * k + 1, FAR, 2 * k + 1, keep)
+
+    def far_back(k, keep=True):
+        for c in range(2, 4):
+            far_slab(k, c).wait()
         for u in range(2):
-            i = 2 * k + u
-            mid(i, u == 0, lambda c: far_slab(i - half, c).start())
+            z_wait(SFAR, 2 * k + u)
+        multiply(4 * k + 2, SFAR, 2 * k, 4 * k + 3, SFAR, 2 * k + 1, keep)
+
+    far_front(0)
+    back(pieces - 1)
 
     z_sent(0, pieces)
     z_sent(1, pieces)
     z_sent(2, pieces)
+
     def again(owner, i):
         return a_copy(owner, i, zbase + i, 2 * pieces + i)
 
     for i in range(4):
         again(me, i).start()
 
-    def far(k, keep):
-        for u in range(2):
-            z_wait(FAR, 2 * k + u)
-            z_copy(FAR, SFAR, 2 * k + u, sib, 7).start()
-        for c in range(4):
-            far_slab(k, c).wait()
-        multiply(4 * k, FAR, 2 * k, 4 * k + 1, FAR, 2 * k + 1, keep)
-        for u in range(2):
-            z_wait(SFAR, 2 * k + u)
-        multiply(4 * k + 2, SFAR, 2 * k, 4 * k + 3, SFAR, 2 * k + 1, keep)
-
-    @pl.loop(0, pieces // 2 - 1)
+    @pl.loop(1, half - 1)
     def _(k):
-        far(k, True)
-
-    far(pieces // 2 - 1, False)
+        far_front(k)
+        far_back(k - 1)
+
+    far_front(half - 1, keep=False)
+    far_back(half - 2)
+    far_back(half - 1, keep=False)
 
     z_sent(3, pieces)
     z_sent(4, pieces)

time: 64.7 us -> 63.9 us (0.988)
  Pallas kernels: 62.8 us -> 62 us
    pallas_call x1, Pallas kernels: 62.8 us -> 62 us  [per_device(): pl.pallas_call(functools.partial(kernel, n), name='gcn', out_shape=jax.Sh...]
where the time goes in v4:
time: 63.9 us; the launch traced here: 63.8 us
  Pallas kernels  62 us (97%)
  local copies, waits for them, and re-layouts  1.77 us (3%)
    pallas_call x1, Pallas kernels, per_device(): pl.pallas_call(functools.partial(kernel, n), name='gcn', out_shape=jax.Sh...  62 us
    unnamed x1, local copies, waits for them, and re-layouts  1.77 us

profile of v4, /device:TPU:112, one launch (start us, length us, event | category | flops | bytes accessed | tf_op | source)
XLA Modules:
  0.0 63.8 jit_solution(9253765867093423058)
XLA Ops:
  0.0 62.0 %gcn.1 = f32[41,2048]{1,0:T(8,128)} custom-call(bf16[2048,16384]{1,0:T(8,128)(2,1)} %a_hbm.1, bf16[602,2048]{1,0:T(8,128)(2,1)} %bitcast.4, bf16[602,256]{1,0:T(8,128)(2,1)} %w0_hbm.1, bf16[41,256]{1,0:T(8,128)(2,1)} %bitcast.5), custom_call_target="tpu_custom_call" | custom-call | flops 19931332608 | bytes 67108864 | tf_op jit(solution)/shard_map/gcn/pallas_call | solution.py:361
  62.0 1.8 %copy.6 = f32[2048,41]{0,1:T(8,128)} copy(f32[2048,41]{0,1:T(8,128)} %bitcast.3) | data formatting | bytes 671744

commit v5 on v4

--- a/solution.py
+++ b/solution.py
@@ -230,13 +230,14 @@
     for i in range(4):
         again(me, i).start()
 
+    far_back(0)
+
     @pl.loop(1, half - 1)
     def _(k):
         far_front(k)
-        far_back(k - 1)
+        far_back(k)
 
     far_front(half - 1, keep=False)
-    far_back(half - 2)
     far_back(half - 1, keep=False)
 
     z_sent(3, pieces)
@@ -259,29 +260,24 @@
     y_copy(OWN, LEFT, 1, right, 1).start()
     y_copy(OWN, RIGHT, 0, left, 2).start()
 
-    def second(work, first=False):
+    def second(streamed, turned, first_streamed=False, first_turned=False):
+        steps = max(len(streamed), 1)
+        per = -(-len(turned) // steps)
         for j in range(pieces):
-            total = None
-            for q, h, i, slot in work:
-                y = jnp.concatenate([z1t[q, h, i], jnp.zeros((LANES - z1t.shape[3], TILE), BF16)], axis=0)
-                term = lax.dot_general(
-                    slab[slot, part(j), :], y, (((1,), (1,)), ((), ())), preferred_element_type=F32)
-                total = term if total is None else total + term
-            if first:
-                acc[part(j), 0:LANES] = total
-            else:
-                acc[part(j), 0:LANES] += total
-
-    def second_turned(work, first=False):
-        for j in range(pieces):
-            total = None
-            for q, h, i, slot in work:
-                term = jnp.dot(z1t[q, h, i], slab[slot, part(j), :], preferred_element_type=F32)
-                total = term if total is None else total + term
-            if first:
-                h2t[j] = total
-            else:
-                h2t[j] += total
+            down = across = None
+            for k in range(steps):
+                for q, h, i, slot in turned[k * per:(k + 1) * per]:
+                    term = jnp.dot(z1t[q, h, i], slab[slot, part(j), :], preferred_element_type=F32)
+                    across = term if across is None else across + term
+                for q, h, i, slot in streamed[k:k + 1]:
+                    y = jnp.concatenate([z1t[q, h, i], jnp.zeros((LANES - z1t.shape[3], TILE), BF16)], axis=0)
+                    term = lax.dot_general(
+                        slab[slot, part(j), :], y, (((1,), (1,)), ((), ())), preferred_element_type=F32)
+                    down = term if down is None else down + term
+            if down is not None:
+                acc[part(j), 0:LANES] = down if first_streamed else acc[part(j), 0:LANES] + down
+            if across is not None:
+                h2t[j] = across if first_turned else h2t[j] + across
 
     def pieces_of(q, h, slot_of):
         return [(q, h, i, slot_of(h * half + i)) for i in range(half)]
@@ -298,7 +294,7 @@
     for h in range(2):
         for i in range(half):
             again(me, h * half + i).wait()
-        second(pieces_of(OWN, h, home), first=h == 0)
+        second(pieces_of(OWN, h, home), [], first_streamed=h == 0)
         for i in range(half):
             again(sib, h * half + i).start()
     y_wait(LEFT, 0)
@@ -307,31 +303,31 @@
     y_wait(RIGHT, 1)
     y_copy(RIGHT, FAR, 1, left, 6).start()
     y_copy(RIGHT, SRIGHT, 1, sib, 4).start()
-    second_turned(pieces_of(LEFT, 0, mid_slot(0)) + pieces_of(RIGHT, 1, mid_slot(1)), first=True)
+    y_wait(SIB, 0)
+    for i in range(half):
+        again(sib, i).wait()
+    second(pieces_of(SIB, 0, home), pieces_of(LEFT, 0, mid_slot(0)) + pieces_of(RIGHT, 1, mid_slot(1)), first_turned=True)
     y_wait(LEFT, 1)
     y_copy(LEFT, SLEFT, 1, sib, 3).start()
     y_wait(RIGHT, 0)
     y_copy(RIGHT, SRIGHT, 0, sib, 4).start()
-    for h in range(2):
-        y_wait(SIB, h)
-    for i in range(pieces):
+    y_wait(SIB, 1)
+    for i in range(half, pieces):
         again(sib, i).wait()
-    second(pieces_of(SIB, 0, home) + pieces_of(SIB, 1, home))
-    second_turned(pieces_of(LEFT, 1, mid_slot(0)) + pieces_of(RIGHT, 0, mid_slot(1)))
+    second(pieces_of(SIB, 1, home), pieces_of(LEFT, 1, mid_slot(0)) + pieces_of(RIGHT, 0, mid_slot(1)))
     for h in range(2):
         y_wait(FAR, h)
         y_copy(FAR, SFAR, h, sib, 7).start()
     for h in range(2):
         y_wait(SLEFT, h)
         y_wait(SRIGHT, 1 - h)
-        second_turned(pieces_of(SLEFT, h, mid_slot(2)) + pieces_of(SRIGHT, 1 - h, mid_slot(3)))
     far_work = pieces_of(FAR, 0, far_slot(0)) + pieces_of(FAR, 1, far_slot(0))
     sfar_work = pieces_of(SFAR, 0, far_slot(1)) + pieces_of(SFAR, 1, far_slot(1))
-    second_turned(far_work[:-2])
+    second([], pieces_of(SLEFT, 0, mid_slot(2)) + pieces_of(SRIGHT, 1, mid_slot(3)))
+    second(far_work[-2:], pieces_of(SLEFT, 1, mid_slot(2)) + pieces_of(SRIGHT, 0, mid_slot(3)) + far_work[:-2])
     for h in range(2):
         y_wait(SFAR, h)
-    second_turned(sfar_work[:-2])
-    second(far_work[-2:] + sfar_work[-2:])
+    second(sfar_work[-2:], sfar_work[:-2])
     for j in range(pieces):
         out_buf[j] = jnp.maximum(h2t[j, 0:classes] + acc[part(j), 0:LANES].T[0:classes], 0.0)
 

time: 63.9 us -> 63.5 us (level)
  no operation moved by 1% of the time
where the time goes in v5:
time: 63.5 us; the launch traced here: 63.4 us
  Pallas kernels  61.6 us (97%)
  local copies, waits for them, and re-layouts  1.77 us (3%)
    pallas_call x1, Pallas kernels, per_device(): pl.pallas_call(functools.partial(kernel, n), name='gcn', out_shape=jax.Sh...  61.6 us
    unnamed x1, local copies, waits for them, and re-layouts  1.77 us

profile of v5, /device:TPU:112, one launch (start us, length us, event | category | flops | bytes accessed | tf_op | source)
XLA Modules:
  0.0 63.4 jit_solution(11338436668022887345)
XLA Ops:
  0.0 61.6 %gcn.1 = f32[41,2048]{1,0:T(8,128)} custom-call(bf16[2048,16384]{1,0:T(8,128)(2,1)} %a_hbm.1, bf16[602,2048]{1,0:T(8,128)(2,1)} %bitcast.4, bf16[602,256]{1,0:T(8,128)(2,1)} %w0_hbm.1, bf16[41,256]{1,0:T(8,128)(2,1)} %bitcast.5), custom_call_target="tpu_custom_call" | custom-call | flops 19931332608 | bytes 67108864 | tf_op jit(solution)/shard_map/gcn/pallas_call | solution.py:357
  61.6 1.8 %copy.6 = f32[2048,41]{0,1:T(8,128)} copy(f32[2048,41]{0,1:T(8,128)} %bitcast.3) | data formatting | bytes 671744

commit v6 on v5

--- a/solution.py
+++ b/solution.py
@@ -100,8 +100,6 @@
     def _(i):
         own_slab(i).start()
 
-    acc[...] = jnp.zeros_like(acc)
-    w1_pad[...] = jnp.zeros_like(w1_pad)
     w0_copy.wait()
 
     def send_own(i):
@@ -119,12 +117,18 @@
             h0_copy(i + H0_RING).start()
 
     feature(0)
+    acc[...] = jnp.zeros_like(acc)
+    w1_pad[...] = jnp.zeros_like(w1_pad)
     pl.semaphore_wait(barrier, 3)
+    send_own(0)
 
     @pl.loop(1, pieces)
     def _(i):
         feature(i)
-        send_own(i - 1)
+
+        @pl.when(i > 1)
+        def _():
+            send_own(i - 1)
 
     @pl.loop(0, pieces)
     def _(i):

time: 63.5 us -> 63.1 us (level)
  no operation moved by 1% of the time
where the time goes in v6:
time: 63.1 us; the launch traced here: 63 us
  Pallas kernels  61.3 us (97%)
  local copies, waits for them, and re-layouts  1.77 us (3%)
    pallas_call x1, Pallas kernels, per_device(): pl.pallas_call(functools.partial(kernel, n), name='gcn', out_shape=jax.Sh...  61.3 us
    unnamed x1, local copies, waits for them, and re-layouts  1.77 us

profile of v6, /device:TPU:112, one launch (start us, length us, event | category | flops | bytes accessed | tf_op | source)
XLA Modules:
  0.0 63.0 jit_solution(3429474131003787736)
XLA Ops:
  0.0 61.3 %gcn.1 = f32[41,2048]{1,0:T(8,128)} custom-call(bf16[2048,16384]{1,0:T(8,128)(2,1)} %a_hbm.1, bf16[602,2048]{1,0:T(8,128)(2,1)} %bitcast.4, bf16[602,256]{1,0:T(8,128)(2,1)} %w0_hbm.1, bf16[41,256]{1,0:T(8,128)(2,1)} %bitcast.5), custom_call_target="tpu_custom_call" | custom-call | flops 19931332608 | bytes 67108864 | tf_op jit(solution)/shard_map/gcn/pallas_call | solution.py:361
  61.3 1.8 %copy.6 = f32[2048,41]{0,1:T(8,128)} copy(f32[2048,41]{0,1:T(8,128)} %bitcast.3) | data formatting | bytes 671744

commit v7 on v6

--- a/solution.py
+++ b/solution.py
@@ -14,7 +14,8 @@
 
 OWN, SIB, SLEFT, SRIGHT, LEFT, RIGHT, FAR, SFAR = range(8)
 BLOCKS = 8
-H0_RING = 4
+H0_RING = 2
+EXTRA = 2
 LANES = 128
 
 
@@ -53,8 +54,12 @@
         slot = 2 * pieces + 4 * i + c
         return a_copy(device(2 * (c % 2) - 1, c // 2), i, slot, slot)
 
+    def far_place(k, c):
+        last = 4 * (half - 1) + 2
+        return 4 * k + c + (c // 2) * (k // (half - 1)) * (zbase - EXTRA - last)
+
     def far_slab(k, c):
-        slot = 4 * k + c
+        slot = far_place(k, c)
         return a_copy(device(2, c // 2), 2 * k + c % 2, slot, slot)
 
     def z_ref(q, i):
@@ -219,7 +224,7 @@
             far_slab(k, c).wait()
         for u in range(2):
             z_wait(SFAR, 2 * k + u)
-        multiply(4 * k + 2, SFAR, 2 * k, 4 * k + 3, SFAR, 2 * k + 1, keep)
+        multiply(far_place(k, 2), SFAR, 2 * k, far_place(k, 3), SFAR, 2 * k + 1, keep)
 
     far_front(0)
     back(pieces - 1)
@@ -293,21 +298,24 @@
         return lambda i: 2 * pieces + 4 * i + c
 
     def far_slot(c):
-        return lambda i: 4 * (i // 2) + 2 * c + i % 2
+        return lambda i: far_place(i // 2, 2 * c + i % 2)
 
     for h in range(2):
         for i in range(half):
             again(me, h * half + i).wait()
         second(pieces_of(OWN, h, home), [], first_streamed=h == 0)
-        for i in range(half):
-            again(sib, h * half + i).start()
+        for i in range(h * half, min((h + 1) * half, pieces - EXTRA)):
+            again(sib, i).start()
+    y_wait(SIB, 0)
+    y_wait(SIB, 1)
+    kept = [(SIB, 1, i % half, pieces + i) for i in range(pieces - EXTRA, pieces)]
+    second(kept, [])
     y_wait(LEFT, 0)
     y_copy(LEFT, FAR, 0, right, 5).start()
     y_copy(LEFT, SLEFT, 0, sib, 3).start()
     y_wait(RIGHT, 1)
     y_copy(RIGHT, FAR, 1, left, 6).start()
     y_copy(RIGHT, SRIGHT, 1, sib, 4).start()
-    y_wait(SIB, 0)
     for i in range(half):
         again(sib, i).wait()
     second(pieces_of(SIB, 0, home), pieces_of(LEFT, 0, mid_slot(0)) + pieces_of(RIGHT, 1, mid_slot(1)), first_turned=True)
@@ -315,10 +323,9 @@
     y_copy(LEFT, SLEFT, 1, sib, 3).start()
     y_wait(RIGHT, 0)
     y_copy(RIGHT, SRIGHT, 0, sib, 4).start()
-    y_wait(SIB, 1)
-    for i in range(half, pieces):
+    for i in range(half, pieces - EXTRA):
         again(sib, i).wait()
-    second(pieces_of(SIB, 1, home), pieces_of(LEFT, 1, mid_slot(0)) + pieces_of(RIGHT, 0, mid_slot(1)))
+    second(pieces_of(SIB, 1, home)[:-EXTRA], pieces_of(LEFT, 1, mid_slot(0)) + pieces_of(RIGHT, 0, mid_slot(1)))
     for h in range(2):
         y_wait(FAR, h)
         y_copy(FAR, SFAR, h, sib, 7).start()
@@ -365,7 +372,7 @@
             in_specs=[pl.BlockSpec(memory_space=pl.ANY)] * 4,
             out_specs=pl.BlockSpec(memory_space=pl.ANY),
             scratch_shapes=[
-                pltpu.VMEM((resident + BLOCKS, rows, TILE), BF16),
+                pltpu.VMEM((resident + EXTRA + BLOCKS, rows, TILE), BF16),
                 pltpu.VMEM((rows, hidden), F32),
                 pltpu.VMEM((H0_RING, feat, TILE), BF16),
                 pltpu.VMEM((feat, hidden), BF16),
@@ -374,7 +381,7 @@
                 pltpu.VMEM((BLOCKS, 2, pieces // 2, padded, TILE), BF16),
                 pltpu.VMEM((pieces, padded, TILE), F32),
                 pltpu.VMEM((pieces, classes, TILE), F32),
-                pltpu.SemaphoreType.DMA((resident,)),
+                pltpu.SemaphoreType.DMA((resident + EXTRA,)),
                 pltpu.SemaphoreType.DMA((H0_RING,)),
                 pltpu.SemaphoreType.DMA((2,)),
                 pltpu.SemaphoreType.DMA((BLOCKS, pieces)),

time: 63.1 us -> 62.8 us (level)
  no operation moved by 1% of the time
where the time goes in v7:
time: 62.8 us; the launch traced here: 62.6 us
  Pallas kernels  60.9 us (97%)
  local copies, waits for them, and re-layouts  1.77 us (3%)
    pallas_call x1, Pallas kernels, per_device(): pl.pallas_call(functools.partial(kernel, n), name='gcn', out_shape=jax.Sh...  60.9 us
    unnamed x1, local copies, waits for them, and re-layouts  1.77 us

profile of v7, /device:TPU:112, one launch (start us, length us, event | category | flops | bytes accessed | tf_op | source)
XLA Modules:
  0.0 62.6 jit_solution(13305076367605484876)
XLA Ops:
  0.0 60.9 %gcn.1 = f32[41,2048]{1,0:T(8,128)} custom-call(bf16[2048,16384]{1,0:T(8,128)(2,1)} %a_hbm.1, bf16[602,2048]{1,0:T(8,128)(2,1)} %bitcast.4, bf16[602,256]{1,0:T(8,128)(2,1)} %w0_hbm.1, bf16[41,256]{1,0:T(8,128)(2,1)} %bitcast.5), custom_call_target="tpu_custom_call" | custom-call | flops 19931332608 | bytes 67108864 | tf_op jit(solution)/shard_map/gcn/pallas_call | solution.py:368
  60.9 1.8 %copy.6 = f32[2048,41]{0,1:T(8,128)} copy(f32[2048,41]{0,1:T(8,128)} %bitcast.3) | data formatting | bytes 671744
